TPU v7x, 256 devices: a whole 4x4x8 slice. The times are simulated.
256 devices in a mesh: slab: 128 (over z, y, x), comp: 2 (over core).
Axes of the slice: x: 4, y: 4, z: 8, core: 2. Of those that a mesh axis runs over, the one named last changes fastest.
Arguments:
- polarization: float32 [6, 128, 128, 128], P('comp', 'slab'), parts along dimension 0, may hold values from -6 to 6
- inverse_polarizability: float32 [128, 128, 128], P('slab'), may hold values from 0.5 to 2
- occupancy: int32 [128, 16, 16], P('slab'), may hold values 0 or 1
- green_fourier: float32 [6, 256, 256, 256], P(None, 'slab'), may hold values from -12 to 12
Outputs:
- first_image: float32 [6, 128, 128, 128], P('comp', 'slab'), parts along dimension 0
- second_image: float32 [6, 128, 128, 128], P('comp', 'slab'), parts along dimension 0
There are 2 independent parts, one for each index of `comp`. A program takes and returns all parts, laid end to end along the dimension named above; an argument that names none is the same for every part. Nothing has to cross between parts.
All inputs are finite; a program needn't handle non-finite values. No bound on the sum of `occupancy` on one device may be relied on, other than what follows from the above.
Results may differ from a plain program's by a relative error of at most 0.0001.
Values sent between devices are 32-bit elements; how exact they have to be, the bound alone decides.
No kernel may reach another device: no remote copies, remote signals or barrier semaphores. Data moves between devices by JAX's collectives and lax.ppermute only.
A program may use at most 64 MiB of HBM per device.

v0:
```python
import functools

import jax
import jax.numpy as jnp
import numpy as np
from jax import lax
from jax.experimental import pallas as pl
from jax.experimental.pallas import tpu as pltpu
from jax.sharding import PartitionSpec as P

BLOCK = 8
F32 = jnp.float32
BF16 = jnp.bfloat16
PARTS = 3
PLANES = 2
PIECES = PARTS * PLANES * 2


def halves_of(table):
    high = table.astype(jnp.bfloat16)
    low = (table - high.astype(np.float64)).astype(jnp.bfloat16)
    return (high, low)


def angles(count_in, count_out):
    phase = np.outer(np.arange(count_in), np.arange(count_out)) % count_out
    return 2.0 * np.pi * phase / count_out


def plane_tables(cells):
    angle = angles(cells, 2 * cells)
    cosine, sine = np.cos(angle), np.sin(angle)
    table = np.block([[cosine, -sine], [sine, cosine]])
    return halves_of(table) + halves_of(np.ascontiguousarray(table.T))


def z_tables(cells, devices):
    angle = angles(cells, 2 * cells)
    per_owner = 2 * cells // devices
    both = np.stack([np.cos(angle).T, -np.sin(angle).T])
    both = both.reshape(2, devices, per_owner, cells).transpose(2, 0, 1, 3)
    table = both.reshape(4 * cells, cells)
    return halves_of(table) + halves_of(np.ascontiguousarray(table.T) / float((2 * cells) ** 3))


def split(value):
    high = value.astype(BF16)
    return (high, (value - high.astype(F32)).astype(BF16))


def dot3(left, right, dims=((1,), (0,))):
    def one(a, b):
        return lax.dot_general(a, b, (dims, ((), ())), preferred_element_type=F32)

    return one(left[0], right[0]) + one(left[1], right[0]) + one(left[0], right[1])


def mask_of(occupancy, cells):
    blocks = occupancy.shape[-1]
    row = lax.broadcasted_iota(jnp.int32, (cells, blocks), 0)
    col = lax.broadcasted_iota(jnp.int32, (cells, blocks), 1)
    expand = jnp.where(row // BLOCK == col, 1.0, 0.0).astype(F32)
    flags = occupancy.astype(F32)
    rows = jnp.dot(expand, flags, preferred_element_type=F32)
    return lax.dot_general(rows, expand, (((1,), (1,)), ((), ())), preferred_element_type=F32)


def put_pieces(out_ref, part, spread, devices):
    for plane in range(PLANES):
        for kind in range(2):
            piece = (part * PLANES + plane) * 2 + kind
            start = (plane * 2 + kind) * devices
            out_ref[pl.ds(piece, devices, stride=PIECES), :] = spread[start : start + devices]


def forward_z_kernel(field_ref, occupancy_ref, high_ref, low_ref, out_ref):
    cells = field_ref.shape[-1]
    devices = out_ref.shape[0] // PIECES
    mask = mask_of(occupancy_ref[0], cells)
    table = (high_ref[...], low_ref[...])
    for part in range(PARTS):
        masked = split(field_ref[part, 0] * mask)
        spread = dot3(table, masked, ((1,), (1,)))
        put_pieces(out_ref, part, spread, devices)


def image_of(part, data_ref, field_ref, inverse_ref, mask, table, devices):
    stack = [
        data_ref[pl.ds((part * PLANES + plane) * 2 + kind, devices, stride=PIECES), :]
        for plane in range(PLANES)
        for kind in range(2)
    ]
    convolved = dot3(table, split(jnp.concatenate(stack, axis=0))).T
    masked = field_ref[part, 0] * mask
    return inverse_ref[0] * masked - mask * convolved


def middle_z_kernel(
    data_ref, field_ref, inverse_ref, occupancy_ref, high_ref, low_ref, back_high_ref, back_low_ref, image_ref, out_ref
):
    cells = field_ref.shape[-1]
    devices = out_ref.shape[0] // PIECES
    mask = mask_of(occupancy_ref[0], cells)
    table = (high_ref[...], low_ref[...])
    back = (back_high_ref[...], back_low_ref[...])
    for part in range(PARTS):
        image = image_of(part, data_ref, field_ref, inverse_ref, mask, back, devices)
        image_ref[part, 0] = image
        spread = dot3(table, split(image * mask), ((1,), (1,)))
        put_pieces(out_ref, part, spread, devices)


def last_z_kernel(data_ref, field_ref, inverse_ref, occupancy_ref, back_high_ref, back_low_ref, image_ref):
    cells = field_ref.shape[-1]
    devices = data_ref.shape[0] // PIECES
    mask = mask_of(occupancy_ref[0], cells)
    back = (back_high_ref[...], back_low_ref[...])
    for part in range(PARTS):
        image_ref[part, 0] = image_of(part, data_ref, field_ref, inverse_ref, mask, back, devices)


def plane_kernel(data_ref, green_ref, high_ref, low_ref, t_high_ref, t_low_ref, out_ref, spectrum_ref):
    devices = data_ref.shape[0] // PIECES
    length = green_ref.shape[-1]
    combos = ((0, 3, 4), (3, 1, 5), (4, 5, 2))
    table = (high_ref[...], low_ref[...])
    table_t = (t_high_ref[...], t_low_ref[...])
    for plane in range(PLANES):

        def piece_of(part, kind):
            return pl.ds((part * PLANES + plane) * 2 + kind, devices, stride=PIECES)

        for part in range(PARTS):
            rows = jnp.concatenate([data_ref[piece_of(part, 0), :], data_ref[piece_of(part, 1), :]], axis=1)
            along_y = dot3(split(rows), table)
            stacked = jnp.concatenate([along_y[:, :length], along_y[:, length:]], axis=0)
            spectrum_ref[part] = dot3(table_t, split(stacked))
        for part in range(PARTS):
            row = combos[part]
            first, second, third = green_ref[row[0], plane], green_ref[row[1], plane], green_ref[row[2], plane]

            def product(kind):
                where = slice(kind * length, (kind + 1) * length)
                return (
                    first * spectrum_ref[0, where] + second * spectrum_ref[1, where] + third * spectrum_ref[2, where]
                )

            field = jnp.concatenate([product(0), product(1)], axis=0)
            along_x = dot3(table, split(field))
            rows = jnp.concatenate([along_x[:devices], along_x[devices:]], axis=1)
            back = dot3(split(rows), table_t)
            out_ref[piece_of(part, 0), :] = back[:, :devices]
            out_ref[piece_of(part, 1), :] = back[:, devices:]


VMEM = pl.BlockSpec(memory_space=pltpu.VMEM)


def call(kernel, outs, args, flops, scratch=()):
    single = not isinstance(outs, tuple)
    moved = sum(a.size * a.dtype.itemsize for a in args)
    return pl.pallas_call(
        kernel,
        out_shape=outs,
        in_specs=[VMEM] * len(args),
        out_specs=VMEM if single else (VMEM,) * len(outs),
        scratch_shapes=list(scratch),
        cost_estimate=pl.CostEstimate(flops=flops, bytes_accessed=moved, transcendentals=0),
        compiler_params=pltpu.CompilerParams(vmem_limit_bytes=48 * 1024 * 1024),
    )(*args)


def exchange(data, devices):
    rows = data.shape[0] // devices
    flat = data.reshape(devices, 1, rows * data.shape[1])
    moved = lax.all_to_all(flat, "slab", split_axis=0, concat_axis=0, tiled=True)
    return moved.reshape(data.shape)


def per_device(devices, polarization, inverse_polarizability, occupancy, green_fourier):
    cells = polarization.shape[-1]
    length = green_fourier.shape[-1]
    z_high, z_low, back_high, back_low = (jnp.asarray(t) for t in z_tables(cells, devices))
    planes = tuple(jnp.asarray(t) for t in plane_tables(cells))
    sent = jax.ShapeDtypeStruct((devices * PIECES, cells), F32)
    image = jax.ShapeDtypeStruct(polarization.shape, F32)
    z_flops = 3 * 2 * PARTS * cells * cells * 2 * length
    plane_flops = 3 * 2 * PARTS * PLANES * (4 * cells * cells * length + 4 * cells * length * length) * 2

    def planes_of(data):
        scratch = (pltpu.VMEM((PARTS, 2 * length, length), F32),)
        return call(plane_kernel, sent, (data, green_fourier) + planes, plane_flops, scratch)

    data = call(forward_z_kernel, sent, (polarization, occupancy, z_high, z_low), z_flops)
    data = exchange(planes_of(exchange(data, devices)), devices)
    first_image, data = call(
        middle_z_kernel,
        (image, sent),
        (data, polarization, inverse_polarizability, occupancy, z_high, z_low, back_high, back_low),
        2 * z_flops,
    )
    data = exchange(planes_of(exchange(data, devices)), devices)
    second_image = call(
        last_z_kernel,
        image,
        (data, first_image, inverse_polarizability, occupancy, back_high, back_low),
        z_flops,
    )
    return (first_image, second_image)


def solution(mesh):
    return jax.shard_map(
        functools.partial(per_device, mesh.shape["slab"]),
        mesh=mesh,
        in_specs=(
            P("comp", "slab", None, None),
            P("slab", None, None),
            P("slab", None, None),
            P(None, "slab", None, None),
        ),
        out_specs=(P("comp", "slab", None, None), P("comp", "slab", None, None)),
        check_vma=False,
    )
```

profile of v0, /device:TPU:1, one launch (start us, length us, event | category | flops | bytes accessed | tf_op | source)
XLA Modules:
  0.0 158.3 jit_solution(3966397880014439095)
XLA Ops:
  0.6 0.0 copy-start
  0.6 0.9 copy-done
  1.6 0.0 copy-start.4
  1.6 0.9 copy-done.4
  2.5 0.0 copy-start.5
  2.5 0.9 copy-done.5
  3.4 0.0 copy-start.8
  3.4 0.7 copy-done.8
  4.1 0.7 shard_map.131
  4.8 39.7 %all_to_all.20 = f32[128,1,1536]{2,1,0:T(1,128)S(1)} all-to-all(f32[128,1,1536]{2,1,0:T(1,128)S(1)} %bitcast.10), channel_id=1, replica_groups=mesh['slab'=128,'comp'=2] {'slab'}, dimensions={0} | all-to-all | bytes 1572864 | tf_op jit(solution)/shard_map/all_to_all | solution.py:176
  44.5 0.0 copy-start.10
  44.5 1.9 %copy-done.10 = f32[6,2,256,256]{3,2,1,0:T(8,128)S(1)} copy-done((f32[6,2,256,256]{3,2,1,0:T(8,128)S(1)}, f32[6,2,256,256]{3,2,1,0:T(8,128)}, u32[]{:S(2)}) %copy-start.10) | copy-done | bytes 3145752
  46.4 0.0 copy-start.12
  46.4 0.9 copy-done.12
  47.3 0.0 copy-start.14
  47.3 0.9 copy-done.14
  48.3 0.0 copy-start.16
  48.3 0.9 copy-done.16
  49.2 0.0 copy-start.18
  49.2 0.9 copy-done.18
  50.2 0.0 copy-start.1
  50.2 0.0 copy-start.2
  50.2 0.0 copy-start.3
  50.2 0.0 copy-start.6
  50.2 7.0 %shard_map.132 = f32[1536,128]{1,0:T(8,128)S(1)} custom-call(f32[1536,128]{1,0:T(8,128)S(1)} %bitcast.14, f32[6,2,256,256]{3,2,1,0:T(8,128)S(1)} %copy-done.10, bf16[256,512]{1,0:T(8,128)(2,1)S(1)} %copy-done.18, bf16[256,512]{1,0:T(8,128)(2,1)S(1)} %copy-done.16, bf16[512,256]{1,0:T(8,128)(2,1)S(1)} %copy-done.14, bf16[512,256]{1,0:T(8,128)(2,1)S(1)} %copy-done.12), custom_call_target="tpu_custom_call" | custom-call | flops 3623878656 | bytes 4980736 | tf_op jit(solution)/shard_map/pallas_call | solution.py:162
  57.2 0.0 copy-start.11
  57.2 0.0 copy-start.13
  57.2 0.0 copy-start.15
  57.2 0.0 copy-start.17
  57.2 0.0 copy-start.19
  57.3 30.5 %all_to_all.21 = f32[128,1,1536]{2,1,0:T(1,128)S(1)} all-to-all(f32[128,1,1536]{2,1,0:T(1,128)S(1)} %bitcast.15), channel_id=1, replica_groups=mesh['slab'=128,'comp'=2] {'slab'}, dimensions={0} | all-to-all | bytes 1572864 | tf_op jit(solution)/shard_map/all_to_all | solution.py:176
  87.8 0.0 copy-done.1
  87.8 0.0 copy-done.2
  87.8 0.0 copy-done.3
  87.8 0.0 copy-done.6
  87.8 1.8 %shard_map.133 = (f32[3,1,128,128]{3,2,1,0:T(8,128)}, f32[1536,128]{1,0:T(8,128)S(1)}) custom-call(f32[1536,128]{1,0:T(8,128)S(1)} %bitcast.8, f32[3,1,128,128]{3,2,1,0:T(8,128)S(1)} %copy-done.1, f32[1,128,128]{2,1,0:T(8,128)S(1)} %copy-done.6, s32[1,16,16]{2,1,0:T(8,128)S(1)} %copy-done.8, bf16[512,128]{1,0:T(8,128)(2,1)S(1)} %copy-done.5, ...), custom_call_target="tpu_custom_call" | custom-call | flops 301989888 | bytes 1573888 | tf_op jit(solution)/shard_map/pallas_call | solution.py:162
  89.6 30.2 %all_to_all.22 = f32[128,1,1536]{2,1,0:T(1,128)S(1)} all-to-all(f32[128,1,1536]{2,1,0:T(1,128)S(1)} %bitcast.11), channel_id=1, replica_groups=mesh['slab'=128,'comp'=2] {'slab'}, dimensions={0} | all-to-all | bytes 1572864 | tf_op jit(solution)/shard_map/all_to_all | solution.py:176
  119.8 0.0 copy-done.11
  119.8 0.0 copy-done.13
  119.8 0.0 copy-done.15
  119.8 0.0 copy-done.17
  119.8 0.0 copy-done.19
  119.8 0.0 copy-start.7
  119.8 0.0 copy-start.9
  119.8 6.7 %shard_map.134 = f32[1536,128]{1,0:T(8,128)S(1)} custom-call(f32[1536,128]{1,0:T(8,128)S(1)} %bitcast.12, f32[6,2,256,256]{3,2,1,0:T(8,128)S(1)} %copy-done.11, bf16[256,512]{1,0:T(8,128)(2,1)S(1)} %copy-done.19, bf16[256,512]{1,0:T(8,128)(2,1)S(1)} %copy-done.17, bf16[512,256]{1,0:T(8,128)(2,1)S(1)} %copy-done.15, bf16[512,256]{1,0:T(8,128)(2,1)S(1)} %copy-done.13), custom_call_target="tpu_custom_call" | custom-call | flops 3623878656 | bytes 4980736 | tf_op jit(solution)/shard_map/pallas_call | solution.py:162
  126.6 30.4 %all_to_all.23 = f32[128,1,1536]{2,1,0:T(1,128)S(1)} all-to-all(f32[128,1,1536]{2,1,0:T(1,128)S(1)} %bitcast.13), channel_id=1, replica_groups=mesh['slab'=128,'comp'=2] {'slab'}, dimensions={0} | all-to-all | bytes 1572864 | tf_op jit(solution)/shard_map/all_to_all | solution.py:176
  157.0 0.0 copy-done.7
  157.0 0.0 copy-done.9
  157.0 1.3 shard_map.135
Async XLA Ops:
  0.6 0.9 copy-start
  1.6 0.9 copy-start.4
  2.5 0.9 copy-start.5
  3.4 0.7 copy-start.8
  44.5 1.9 %copy-start.10 = (f32[6,2,256,256]{3,2,1,0:T(8,128)S(1)}, f32[6,2,256,256]{3,2,1,0:T(8,128)}, u32[]{:S(2)}) copy-start(f32[6,2,256,256]{3,2,1,0:T(8,128)} %green_ref.3) | copy-start | bytes 9437188
  46.4 0.9 copy-start.12
  47.3 0.9 copy-start.14
  48.3 0.9 copy-start.16
  49.2 0.9 copy-start.18
  50.2 37.6 %copy-start.1 = (f32[3,1,128,128]{3,2,1,0:T(8,128)S(1)}, f32[3,1,128,128]{3,2,1,0:T(8,128)}, u32[]{:S(2)}) copy-start(f32[3,1,128,128]{3,2,1,0:T(8,128)} %field_ref.3) | copy-start | bytes 589828
  50.2 37.6 %copy-start.2 = (bf16[128,512]{1,0:T(8,128)(2,1)S(1)}, bf16[128,512]{1,0:T(8,128)(2,1)}, u32[]{:S(2)}) copy-start(bf16[128,512]{1,0:T(8,128)(2,1)} %constant.19.clone.back_low_ref) | copy-start | bytes 393220
  50.2 37.6 %copy-start.3 = (bf16[128,512]{1,0:T(8,128)(2,1)S(1)}, bf16[128,512]{1,0:T(8,128)(2,1)}, u32[]{:S(2)}) copy-start(bf16[128,512]{1,0:T(8,128)(2,1)} %constant.18.clone.back_high_ref) | copy-start | bytes 393220
  50.2 37.6 %copy-start.6 = (f32[1,128,128]{2,1,0:T(8,128)S(1)}, f32[1,128,128]{2,1,0:T(8,128)}, u32[]{:S(2)}) copy-start(f32[1,128,128]{2,1,0:T(8,128)} %inverse_ref.3) | copy-start | bytes 196612
  57.2 62.6 %copy-start.11 = (f32[6,2,256,256]{3,2,1,0:T(8,128)S(1)}, f32[6,2,256,256]{3,2,1,0:T(8,128)}, u32[]{:S(2)}) copy-start(f32[6,2,256,256]{3,2,1,0:T(8,128)} %green_ref.3) | copy-start | bytes 9437188
  57.2 62.6 %copy-start.13 = (bf16[512,256]{1,0:T(8,128)(2,1)S(1)}, bf16[512,256]{1,0:T(8,128)(2,1)}, u32[]{:S(2)}) copy-start(bf16[512,256]{1,0:T(8,128)(2,1)} %constant.23.clone.t_low_ref) | copy-start | bytes 786436
  57.2 62.6 %copy-start.15 = (bf16[512,256]{1,0:T(8,128)(2,1)S(1)}, bf16[512,256]{1,0:T(8,128)(2,1)}, u32[]{:S(2)}) copy-start(bf16[512,256]{1,0:T(8,128)(2,1)} %constant.22.clone.t_high_ref) | copy-start | bytes 786436
  57.2 62.6 %copy-start.17 = (bf16[256,512]{1,0:T(8,128)(2,1)S(1)}, bf16[256,512]{1,0:T(8,128)(2,1)}, u32[]{:S(2)}) copy-start(bf16[256,512]{1,0:T(8,128)(2,1)} %constant.21.clone.low_ref) | copy-start | bytes 786436
  57.2 62.6 %copy-start.19 = (bf16[256,512]{1,0:T(8,128)(2,1)S(1)}, bf16[256,512]{1,0:T(8,128)(2,1)}, u32[]{:S(2)}) copy-start(bf16[256,512]{1,0:T(8,128)(2,1)} %constant.20.clone.high_ref) | copy-start | bytes 786436
  119.8 37.2 %copy-start.7 = (f32[3,1,128,128]{3,2,1,0:T(8,128)S(1)}, f32[3,1,128,128]{3,2,1,0:T(8,128)}, u32[]{:S(2)}) copy-start(f32[3,1,128,128]{3,2,1,0:T(8,128)} %get-tuple-element.2.field_ref) | copy-start | bytes 589828
  119.8 37.2 %copy-start.9 = (s32[1,16,16]{2,1,0:T(8,128)S(1)}, s32[1,16,16]{2,1,0:T(8,128)}, u32[]{:S(2)}) copy-start(s32[1,16,16]{2,1,0:T(8,128)} %occupancy_ref.5) | copy-start | bytes 3076
where the time goes:
time: 161 us; the launch traced here: 158 us
  blocking collectives  131 us (81%)
  Pallas kernels  17.6 us (11%)
  local copies, waits for them, and re-layouts  9.17 us (6%)
    all_to_all x4, blocking collectives, exchange(): lax.all_to_all(flat, 'slab', split_axis=0, concat_axis=0, tiled=True)  131 us
    pallas_call x5, Pallas kernels, call(): pl.pallas_call(kernel, out_shape=outs, in_specs=[VMEM] * len(args), out_s...  17.6 us
    unnamed x40, local copies, waits for them, and re-layouts  9.17 us

commit v1 on v0

v1 whole, which is shorter than its diff:
```python
import functools

import jax
import jax.numpy as jnp
import numpy as np
from jax import lax
from jax.experimental import pallas as pl
from jax.experimental.pallas import tpu as pltpu
from jax.sharding import PartitionSpec as P


BLOCK = 8
F32 = jnp.float32
BF16 = jnp.bfloat16
PARTS = 3
PIECES = PARTS * 2
COMBOS = ((0, 3, 4), (3, 1, 5), (4, 5, 2))


def halves_of(table):
    high = table.astype(jnp.bfloat16)
    low = (table - high.astype(np.float64)).astype(jnp.bfloat16)
    return (high, low)


def plane_tables(cells):
    phase = np.outer(np.arange(cells), np.arange(2 * cells)) % (2 * cells)
    angle = np.pi * phase / cells
    cosine, sine = np.cos(angle), np.sin(angle)
    table = np.block([[cosine, -sine], [sine, cosine]])
    return halves_of(table) + halves_of(np.ascontiguousarray(table.T))


def kept_plane(owner, devices):
    return 0 if owner < devices // 2 else 1


def pair_of(owner, devices):
    if owner < devices // 2:
        return devices - 1 - owner
    return devices - owner if owner > devices // 2 else 0


def z_tables(cells, devices):
    wave = np.array([2 * d + kept_plane(d, devices) for d in range(devices)])
    angle = np.pi * (np.outer(wave, np.arange(cells)) % (2 * cells)) / cells
    both = np.stack([np.cos(angle), -np.sin(angle)])
    both[1, 0] = np.cos(np.pi * np.arange(cells))
    table = both.reshape(2 * devices, cells)
    return halves_of(table) + halves_of(np.ascontiguousarray(table.T) / float((2 * cells) ** 3))


def split(value):
    high = value.astype(BF16)
    return (high, (value - high.astype(F32)).astype(BF16))


def dot(left, right, dims=((1,), (0,))):
    return lax.dot_general(left, right, (dims, ((), ())), preferred_element_type=F32)


def dot3(left, right, dims=((1,), (0,))):
    return dot(left[0], right[0], dims) + dot(left[1], right[0], dims) + dot(left[0], right[1], dims)


def mask_of(occupancy, cells):
    blocks = occupancy.shape[-1]
    row = lax.broadcasted_iota(jnp.int32, (cells, blocks), 0)
    col = lax.broadcasted_iota(jnp.int32, (cells, blocks), 1)
    expand = jnp.where(row // BLOCK == col, 1.0, 0.0).astype(F32)
    return dot(dot(expand, occupancy.astype(F32)), expand, ((1,), (1,)))


def put_pieces(out_ref, part, spread, devices):
    for kind in range(2):
        out_ref[pl.ds(part * 2 + kind, devices, stride=PIECES), :] = spread[kind * devices : (kind + 1) * devices]


def get_pieces(data_ref, part, devices, axis):
    pieces = [data_ref[pl.ds(part * 2 + kind, devices, stride=PIECES), :] for kind in range(2)]
    return jnp.concatenate(pieces, axis=axis)


def copies_of(pairs, semaphores):
    copies = [pltpu.make_async_copy(src, dst, semaphores.at[i]) for i, (src, dst) in enumerate(pairs)]
    for copy in copies:
        copy.start()
    return copies


def forward_z_kernel(*refs):
    sources, out_ref, (field_ref, occupancy_ref, high_ref, low_ref), semaphores = refs[:4], refs[4], refs[5:9], refs[9]
    for copy in copies_of(list(zip(sources, refs[5:9])), semaphores):
        copy.wait()
    cells = field_ref.shape[-1]
    devices = out_ref.shape[0] // PIECES
    mask = mask_of(occupancy_ref[0], cells)
    table = (high_ref[...], low_ref[...])
    for part in range(PARTS):
        spread = dot3(table, split(field_ref[part, 0] * mask), ((1,), (1,)))
        put_pieces(out_ref, part, spread, devices)


def image_of(part, data_ref, field_ref, inverse_ref, mask, table, devices):
    convolved = dot3(table, split(get_pieces(data_ref, part, devices, 0))).T
    masked = field_ref[part, 0] * mask
    return inverse_ref[0] * masked - mask * convolved


def middle_z_kernel(
    data_ref, field_ref, inverse_ref, occupancy_ref, high_ref, low_ref, back_high_ref, back_low_ref, image_ref, out_ref
):
    cells = field_ref.shape[-1]
    devices = out_ref.shape[0] // PIECES
    mask = mask_of(occupancy_ref[0], cells)
    table = (high_ref[...], low_ref[...])
    back = (back_high_ref[...], back_low_ref[...])
    for part in range(PARTS):
        image = image_of(part, data_ref, field_ref, inverse_ref, mask, back, devices)
        image_ref[part, 0] = image
        spread = dot3(table, split(image * mask), ((1,), (1,)))
        put_pieces(out_ref, part, spread, devices)


def last_z_kernel(data_ref, field_ref, inverse_ref, occupancy_ref, back_high_ref, back_low_ref, image_ref):
    cells = field_ref.shape[-1]
    devices = data_ref.shape[0] // PIECES
    mask = mask_of(occupancy_ref[0], cells)
    back = (back_high_ref[...], back_low_ref[...])
    for part in range(PARTS):
        image_ref[part, 0] = image_of(part, data_ref, field_ref, inverse_ref, mask, back, devices)


def pair_kernel(
    green_ref, mine_hbm, other_hbm, sum_ref, difference_ref, own_ref, mine_ref, other_ref, semaphores, *, devices
):
    length = own_ref.shape[-1]
    slab = lax.axis_index("slab")
    first = slab == 0
    kept = jnp.where(slab >= devices // 2, 1, 0)
    pairs = [(green_ref.at[:, kept], own_ref), (mine_hbm, mine_ref), (other_hbm, other_ref)]
    for copy in copies_of(pairs, semaphores):
        copy.wait()
    core = lax.axis_index("comp")
    row = lax.broadcasted_iota(jnp.int32, (length, length), 0)
    col = lax.broadcasted_iota(jnp.int32, (length, length), 1)
    flip = jnp.where((row + col == length) | (row + col == 0), 1.0, 0.0).astype(BF16)

    def flipped(value):
        high, low = split(value)

        def one(half):
            return dot(flip, dot(half, flip).astype(BF16))

        return one(high) + one(low)

    for here in range(PARTS):
        for received, start in ((mine_ref, core * PARTS), (other_ref, (1 - core) * PARTS)):
            entry = start + here
            own = own_ref[entry]
            pair = received[here, 0]
            pair_flipped = flipped(pair)

            @pl.when(jnp.logical_not(first))
            def _():
                sum_ref[entry] = own + pair_flipped

            @pl.when(first)
            def _():
                own_both = own + flipped(own)
                pair_both = pair + pair_flipped
                sum_ref[entry] = 0.25 * (own_both + pair_both)
                difference_ref[entry] = 0.25 * (own_both - pair_both)


def plane_kernel(data_ref, *refs):
    sources, out_ref, buffers = refs[:6], refs[6], refs[7:13]
    spectrum_ref, field_ref, semaphores = refs[13:]
    tables, (sum_ref, difference_ref) = buffers[:4], buffers[4:]
    copies = copies_of(list(zip(sources[:5], buffers[:5])), semaphores)
    devices = data_ref.shape[0] // PIECES
    length = sum_ref.shape[-1]
    for copy in copies[:4]:
        copy.wait()
    table = (tables[0][...], tables[1][...])
    table_t = (tables[2][...], tables[3][...])

    def transform(sign):
        for part in range(PARTS):
            rows = get_pieces(data_ref, part, devices, 1)
            if sign < 0:
                rows = jnp.concatenate([rows[:, :devices], -rows[:, devices:]], axis=1)
            along_y = dot3(split(rows), table)
            stacked = jnp.concatenate([along_y[:, :length], along_y[:, length:]], axis=0)
            spectrum_ref[part] = dot3(table_t, split(stacked))

    def product(green_ref, part, kind):
        where = slice(kind * length, (kind + 1) * length)
        first, second, third = COMBOS[part]
        return (
            green_ref[first] * spectrum_ref[0, where]
            + green_ref[second] * spectrum_ref[1, where]
            + green_ref[third] * spectrum_ref[2, where]
        )

    transform(1)
    copies[4].wait()
    for part in range(PARTS):
        for kind in range(2):
            field_ref[part, kind * length : (kind + 1) * length] = product(sum_ref, part, kind)

    @pl.when(lax.axis_index("slab") == 0)
    def _():
        copy = pltpu.make_async_copy(sources[5], difference_ref, semaphores.at[5])
        copy.start()
        transform(-1)
        copy.wait()
        for part in range(PARTS):
            for kind in range(2):
                field_ref[part, kind * length : (kind + 1) * length] += product(difference_ref, part, kind)

    for part in range(PARTS):
        along_x = dot3(table, split(field_ref[part]))
        rows = jnp.concatenate([along_x[:devices], along_x[devices:]], axis=1)
        back = dot3(split(rows), table_t)
        for kind in range(2):
            out_ref[pl.ds(part * 2 + kind, devices, stride=PIECES), :] = back[:, kind * devices : (kind + 1) * devices]


VMEM = pl.BlockSpec(memory_space=pltpu.VMEM)
ANY = pl.BlockSpec(memory_space=pltpu.HBM)


def buffers_for(arrays):
    return [pltpu.VMEM(a.shape, a.dtype) for a in arrays]


def call(kernel, outs, args, flops, scratch=(), mebibytes=8, specs=None):
    single = not isinstance(outs, tuple)
    moved = sum(a.size * a.dtype.itemsize for a in args)
    return pl.pallas_call(
        kernel,
        out_shape=outs,
        in_specs=specs or [VMEM] * len(args),
        out_specs=VMEM if single else (VMEM,) * len(outs),
        scratch_shapes=list(scratch),
        cost_estimate=pl.CostEstimate(flops=flops, bytes_accessed=moved, transcendentals=0),
        compiler_params=pltpu.CompilerParams(vmem_limit_bytes=mebibytes * 1024 * 1024),
    )(*args)


def exchange(data, devices):
    rows = data.shape[0] // devices
    flat = data.reshape(devices, 1, rows * data.shape[1])
    moved = lax.all_to_all(flat, "slab", split_axis=0, concat_axis=0, tiled=True)
    return moved.reshape(data.shape)


def per_device(devices, polarization, inverse_polarizability, occupancy, green_fourier):
    cells = polarization.shape[-1]
    length = green_fourier.shape[-1]
    slab, core = lax.axis_index("slab"), lax.axis_index("comp")
    kept = (slab >= devices // 2).astype(jnp.int32)
    given = lax.dynamic_slice(green_fourier, (core * PARTS, 1 - kept, 0, 0), (PARTS, 1, length, length))
    mine = lax.ppermute(given, "slab", [(d, pair_of(d, devices)) for d in range(devices)])
    other = lax.ppermute(mine, "comp", [(0, 1), (1, 0)])

    z_high, z_low, back_high, back_low = (jnp.asarray(t) for t in z_tables(cells, devices))
    planes = tuple(jnp.asarray(t) for t in plane_tables(cells))
    sent = jax.ShapeDtypeStruct((devices * PIECES, cells), F32)
    image = jax.ShapeDtypeStruct(polarization.shape, F32)
    green = jax.ShapeDtypeStruct((2 * PARTS, length, length), F32)
    z_flops = 3 * 2 * PARTS * cells * cells * length
    plane_flops = 3 * 2 * PARTS * (4 * cells * cells * length + 4 * cells * length * length) * 2

    args = (polarization, occupancy, z_high, z_low)
    scratch = buffers_for(args) + [pltpu.SemaphoreType.DMA((4,))]
    data = call(forward_z_kernel, sent, args, z_flops, scratch, specs=[ANY] * 4)
    data = exchange(data, devices)
    args = (green_fourier, mine, other)
    scratch = [pltpu.VMEM(green.shape, F32)] + buffers_for(args[1:]) + [pltpu.SemaphoreType.DMA((3,))]
    pairing = functools.partial(pair_kernel, devices=devices)
    greens = call(pairing, (green, green), args, 4 * 2 * 2 * PARTS * length**3, scratch, 16, [ANY] * 3)

    def planes_of(data):
        args = planes + tuple(greens)
        scratch = buffers_for(args) + [pltpu.VMEM((PARTS, 2 * length, length), F32)] * 2
        scratch = scratch + [pltpu.SemaphoreType.DMA((6,))]
        return call(plane_kernel, sent, (data,) + args, plane_flops, scratch, 24, [VMEM] + [ANY] * 6)

    data = exchange(planes_of(data), devices)
    first_image, data = call(
        middle_z_kernel,
        (image, sent),
        (data, polarization, inverse_polarizability, occupancy, z_high, z_low, back_high, back_low),
        2 * z_flops,
    )
    data = exchange(planes_of(exchange(data, devices)), devices)
    second_image = call(
        last_z_kernel,
        image,
        (data, first_image, inverse_polarizability, occupancy, back_high, back_low),
        z_flops,
    )
    return (first_image, second_image)


def solution(mesh):
    def body(*args):
        return per_device(mesh.shape["slab"], *args)

    return jax.shard_map(
        body,
        mesh=mesh,
        in_specs=(
            P("comp", "slab", None, None),
            P("slab", None, None),
            P("slab", None, None),
            P(None, "slab", None, None),
        ),
        out_specs=(P("comp", "slab", None, None), P("comp", "slab", None, None)),
        check_vma=False,
    )
```

time: 161 us -> 172 us (1.068)
  the two profiles are of different devices: /device:TPU:1 before, /device:TPU:2 now
where the time goes in v1:
time: 172 us; the launch traced here: 171 us
  blocking collectives  68.6 us (40%)
  waiting for transfers between devices  46.3 us (27%)
  starting transfers between devices  26.8 us (16%)
  Pallas kernels  16 us (9%)
  local copies, waits for them, and re-layouts  12.8 us (7%)
    all_to_all x3, blocking collectives, exchange(): lax.all_to_all(flat, 'slab', split_axis=0, concat_axis=0, tiled=True)  68.6 us
    ppermute x1, waiting for transfers between devices, per_device(): lax.ppermute(given, 'slab', [(d, pair_of(d, devices)) for d in range(devi...  35 us
    all_to_all x1, starting transfers between devices, exchange(): lax.all_to_all(flat, 'slab', split_axis=0, concat_axis=0, tiled=True)  17.5 us
    pallas_call x6, Pallas kernels, call(): pl.pallas_call(kernel, out_shape=outs, in_specs=specs or [VMEM] * len(arg...  16 us
    unnamed x46, local copies, waits for them, and re-layouts  11.6 us
    all_to_all x1, waiting for transfers between devices, exchange(): lax.all_to_all(flat, 'slab', split_axis=0, concat_axis=0, tiled=True)  11.3 us
    ppermute x1, starting transfers between devices, per_device(): lax.ppermute(given, 'slab', [(d, pair_of(d, devices)) for d in range(devi...  9.31 us
  transfers between devices with their start and end apart: 3, of which 2 were waited for; matrix products, arithmetic and copies ran while one was open for 0% of the time, Pallas kernels for 3%

profile of v1, /device:TPU:2, one launch (start us, length us, event | category | flops | bytes accessed | tf_op | source)
XLA Modules:
  0.0 171.4 jit_solution(16913109644226418113)
XLA Ops:
  0.6 1.2 constant_dynamic-slice_fusion
  1.8 9.3 %collective-permute-start = (f32[3,1,256,256]{3,2,1,0:T(8,128)S(1)}, f32[3,1,256,256]{3,2,1,0:T(8,128)S(1)}, u32[]{:S(2)}, u32[]{:S(2)}) collective-permute-start(f32[3,1,256,256]{3,2,1,0:T(8,128)S(1)} %constant_dynamic-slice_fusion), channel_id=1, source_target_pairs={{0,254},{2,252},{4,250},{6,248},{8,246},{10,244},{12,242},{14,240}... | collective-permute-start | bytes 2359304 | tf_op jit(solution)/shard_map/ppermute | solution.py:265
  11.1 35.0 %collective-permute-done.mine_hbm = f32[3,1,256,256]{3,2,1,0:T(8,128)S(1)} collective-permute-done((f32[3,1,256,256]{3,2,1,0:T(8,128)S(1)}, f32[3,1,256,256]{3,2,1,0:T(8,128)S(1)}, u32[]{:S(2)}, u32[]{:S(2)}) %collective-permute-start) | collective-permute-done | bytes 786464 | tf_op jit(solution)/shard_map/ppermute | solution.py:265
  46.2 0.0 collective-permute-start.1
  46.2 0.0 copy-start.1
  46.2 0.9 copy-done.1
  47.1 0.0 copy-start.3
  47.1 0.8 copy-done.3
  47.9 0.0 copy-start.5
  47.9 0.8 copy-done.5
  48.8 0.0 copy-start.11
  48.8 0.7 copy-done.11
  49.5 1.8 %shard_map.131 = f32[768,128]{1,0:T(8,128)} custom-call(f32[3,1,128,128]{3,2,1,0:T(8,128)S(1)} %copy-done.1, s32[1,16,16]{2,1,0:T(8,128)S(1)} %copy-done.11, bf16[256,128]{1,0:T(8,128)(2,1)S(1)} %copy-done.3, bf16[256,128]{1,0:T(8,128)(2,1)S(1)} %copy-done.5), custom_call_target="tpu_custom_call" | custom-call | flops 75497472 | bytes 328704 | tf_op jit(solution)/shard_map/pallas_call | solution.py:241
  51.3 17.5 %all-to-all-start = ((f32[128,1,768]{2,1,0:T(1,128)}), f32[128,1,768]{2,1,0:T(1,128)S(1)}, u32[]{:S(2)}, u32[]{:S(2)}) async-start(f32[128,1,768]{2,1,0:T(1,128)} %bitcast), calls=%async_computation | async-start | bytes 786432 | tf_op jit(solution)/shard_map/all_to_all | solution.py:255
  68.8 0.0 collective-permute-done.1.other_hbm
  68.8 0.0 copy-start
  68.8 1.9 %copy-done = f32[6,2,256,256]{3,2,1,0:T(8,128)S(1)} copy-done((f32[6,2,256,256]{3,2,1,0:T(8,128)S(1)}, f32[6,2,256,256]{3,2,1,0:T(8,128)}, u32[]{:S(2)}) %copy-start) | copy-done | bytes 3145752
  70.7 3.6 %shard_map.132 = (f32[6,256,256]{2,1,0:T(8,128)S(1)}, f32[6,256,256]{2,1,0:T(8,128)S(1)}) custom-call(f32[6,2,256,256]{3,2,1,0:T(8,128)S(1)} %copy-done, f32[3,1,256,256]{3,2,1,0:T(8,128)S(1)} %collective-permute-done.mine_hbm, f32[3,1,256,256]{3,2,1,0:T(8,128)S(1)} %collective-permute-done.1.other_hbm), custom_call_target="tpu_custom_call" | custom-call | flops 805306368 | bytes 4718592 | tf_op jit(solution)/shard_map/pallas_call | solution.py:241
  74.3 0.0 copy-start.13
  74.3 1.2 copy-done.13
  75.4 11.3 %all-to-all-done = f32[128,1,768]{2,1,0:T(1,128)S(1)} async-done(((f32[128,1,768]{2,1,0:T(1,128)}), f32[128,1,768]{2,1,0:T(1,128)S(1)}, u32[]{:S(2)}, u32[]{:S(2)}) %all-to-all-start) | async-done | bytes 393248 | tf_op jit(solution)/shard_map/all_to_all | solution.py:255
  86.8 0.0 copy-start.14
  86.8 1.4 copy-done.14
  88.2 0.0 copy-start.15
  88.2 0.9 copy-done.15
  89.1 0.0 copy-start.17
  89.1 0.9 copy-done.17
  90.1 0.0 copy-start.19
  90.1 0.9 copy-done.19
  91.0 0.0 copy-start.21
  91.0 0.9 copy-done.21
  92.0 0.0 copy-start.2
  92.0 0.0 copy-start.4
  92.0 0.0 copy-start.6
  92.0 0.0 copy-start.7
  92.0 0.0 copy-start.8
  92.0 0.0 copy-start.9
  92.0 0.0 copy-start.12
  92.0 0.0 copy-start.16
  92.0 0.0 copy-start.18
  92.0 0.0 copy-start.20
  92.1 0.0 copy-start.22
  92.1 4.1 %shard_map.133 = f32[768,128]{1,0:T(8,128)S(1)} custom-call(f32[768,128]{1,0:T(8,128)S(1)} %bitcast.10, bf16[256,512]{1,0:T(8,128)(2,1)S(1)} %copy-done.15, bf16[256,512]{1,0:T(8,128)(2,1)S(1)} %copy-done.17, bf16[512,256]{1,0:T(8,128)(2,1)S(1)} %copy-done.19, bf16[512,256]{1,0:T(8,128)(2,1)S(1)} %copy-done.21, f32[6,256,256]{2,1,0:T(8,128)S(1)} %get-tuple-element.6.refs_4_, ...), custom_call_target="tpu_custom_call" | custom-call | flops 1811939328 | bytes 4587520 | tf_op jit(solution)/shard_map/pallas_call | solution.py:241
  96.2 24.3 %all_to_all.20 = f32[128,1,768]{2,1,0:T(1,128)S(1)} all-to-all(f32[128,1,768]{2,1,0:T(1,128)S(1)} %bitcast.14), channel_id=1, replica_groups=mesh['slab'=128,'comp'=2] {'slab'}, dimensions={0} | all-to-all | bytes 786432 | tf_op jit(solution)/shard_map/all_to_all | solution.py:255
  120.5 0.0 copy-done.2
  120.5 0.0 copy-done.4
  120.5 0.0 copy-done.6
  120.5 0.0 copy-done.7
  120.5 0.0 copy-done.8
  120.5 0.0 copy-done.9
  120.5 0.0 copy-done.12
  120.5 1.3 shard_map.134
  121.8 21.7 %all_to_all.21 = f32[128,1,768]{2,1,0:T(1,128)S(1)} all-to-all(f32[128,1,768]{2,1,0:T(1,128)S(1)} %bitcast.13), channel_id=1, replica_groups=mesh['slab'=128,'comp'=2] {'slab'}, dimensions={0} | all-to-all | bytes 786432 | tf_op jit(solution)/shard_map/all_to_all | solution.py:255
  143.5 0.0 copy-done.16
  143.5 0.0 copy-done.18
  143.5 0.0 copy-done.20
  143.5 0.0 copy-done.22
  143.5 0.0 copy-start.10
  143.5 4.1 %shard_map.135 = f32[768,128]{1,0:T(8,128)S(1)} custom-call(f32[768,128]{1,0:T(8,128)S(1)} %bitcast.11, bf16[256,512]{1,0:T(8,128)(2,1)S(1)} %copy-done.16, bf16[256,512]{1,0:T(8,128)(2,1)S(1)} %copy-done.18, bf16[512,256]{1,0:T(8,128)(2,1)S(1)} %copy-done.20, bf16[512,256]{1,0:T(8,128)(2,1)S(1)} %copy-done.22, f32[6,256,256]{2,1,0:T(8,128)S(1)} %get-tuple-element.6.refs_4_, ...), custom_call_target="tpu_custom_call" | custom-call | flops 1811939328 | bytes 4587520 | tf_op jit(solution)/shard_map/pallas_call | solution.py:241
  147.6 22.6 %all_to_all.22 = f32[128,1,768]{2,1,0:T(1,128)S(1)} all-to-all(f32[128,1,768]{2,1,0:T(1,128)S(1)} %bitcast.12), channel_id=1, replica_groups=mesh['slab'=128,'comp'=2] {'slab'}, dimensions={0} | all-to-all | bytes 786432 | tf_op jit(solution)/shard_map/all_to_all | solution.py:255
  170.3 0.0 copy-done.10
  170.3 1.1 shard_map.136
Async XLA Ops:
  1.8 44.3 %collective-permute-start = (f32[3,1,256,256]{3,2,1,0:T(8,128)S(1)}, f32[3,1,256,256]{3,2,1,0:T(8,128)S(1)}, u32[]{:S(2)}, u32[]{:S(2)}) collective-permute-start(f32[3,1,256,256]{3,2,1,0:T(8,128)S(1)} %constant_dynamic-slice_fusion), channel_id=1, source_target_pairs={{0,254},{2,252},{4,250},{6,248},{8,246},{10,244},{12,242},{14,240}... | collective-permute-start | bytes 2359304 | tf_op jit(solution)/shard_map/ppermute | solution.py:265
  46.2 22.6 %collective-permute-start.1 = (f32[3,1,256,256]{3,2,1,0:T(8,128)S(1)}, f32[3,1,256,256]{3,2,1,0:T(8,128)S(1)}, u32[]{:S(2)}, u32[]{:S(2)}) collective-permute-start(f32[3,1,256,256]{3,2,1,0:T(8,128)S(1)} %collective-permute-done.mine_hbm), channel_id=1, source_target_pairs={{0,1},{1,0},{2,3},{3,2},{4,5},{5,4},{6,7},{7,6},{8,9},{9,8},{10,11... | collective-permute-start | bytes 2359304 | tf_op jit(solution)/shard_map/ppermute | solution.py:266
  46.2 0.9 copy-start.1
  47.1 0.8 copy-start.3
  47.9 0.8 copy-start.5
  48.8 0.7 copy-start.11
  51.3 35.5 %all-to-all-start = ((f32[128,1,768]{2,1,0:T(1,128)}), f32[128,1,768]{2,1,0:T(1,128)S(1)}, u32[]{:S(2)}, u32[]{:S(2)}) async-start(f32[128,1,768]{2,1,0:T(1,128)} %bitcast), calls=%async_computation | async-start | bytes 786432 | tf_op jit(solution)/shard_map/all_to_all | solution.py:255
  68.8 1.9 %copy-start = (f32[6,2,256,256]{3,2,1,0:T(8,128)S(1)}, f32[6,2,256,256]{3,2,1,0:T(8,128)}, u32[]{:S(2)}) copy-start(f32[6,2,256,256]{3,2,1,0:T(8,128)} %green_ref.1) | copy-start | bytes 9437188
  74.3 1.2 copy-start.13
  86.8 1.4 copy-start.14
  88.2 0.9 copy-start.15
  89.1 0.9 copy-start.17
  90.1 0.9 copy-start.19
  91.0 0.9 copy-start.21
  92.0 28.5 %copy-start.2 = (f32[3,1,128,128]{3,2,1,0:T(8,128)S(1)}, f32[3,1,128,128]{3,2,1,0:T(8,128)}, u32[]{:S(2)}) copy-start(f32[3,1,128,128]{3,2,1,0:T(8,128)} %field_ref.1) | copy-start | bytes 589828
  92.0 28.5 %copy-start.4 = (bf16[256,128]{1,0:T(8,128)(2,1)S(1)}, bf16[256,128]{1,0:T(8,128)(2,1)}, u32[]{:S(2)}) copy-start(bf16[256,128]{1,0:T(8,128)(2,1)} %constant.36.clone.refs_2_.high_ref) | copy-start | bytes 196612
  92.0 28.5 %copy-start.6 = (bf16[256,128]{1,0:T(8,128)(2,1)S(1)}, bf16[256,128]{1,0:T(8,128)(2,1)}, u32[]{:S(2)}) copy-start(bf16[256,128]{1,0:T(8,128)(2,1)} %constant.37.clone.refs_3_.low_ref) | copy-start | bytes 196612
  92.0 28.5 %copy-start.7 = (f32[1,128,128]{2,1,0:T(8,128)S(1)}, f32[1,128,128]{2,1,0:T(8,128)}, u32[]{:S(2)}) copy-start(f32[1,128,128]{2,1,0:T(8,128)} %inverse_ref.3) | copy-start | bytes 196612
  92.0 28.5 %copy-start.8 = (bf16[128,256]{1,0:T(8,128)(2,1)S(1)}, bf16[128,256]{1,0:T(8,128)(2,1)}, u32[]{:S(2)}) copy-start(bf16[128,256]{1,0:T(8,128)(2,1)} %constant.38.clone.back_high_ref) | copy-start | bytes 196612
  92.0 28.5 %copy-start.9 = (bf16[128,256]{1,0:T(8,128)(2,1)S(1)}, bf16[128,256]{1,0:T(8,128)(2,1)}, u32[]{:S(2)}) copy-start(bf16[128,256]{1,0:T(8,128)(2,1)} %constant.39.clone.back_low_ref) | copy-start | bytes 196612
  92.0 28.5 %copy-start.12 = (s32[1,16,16]{2,1,0:T(8,128)S(1)}, s32[1,16,16]{2,1,0:T(8,128)}, u32[]{:S(2)}) copy-start(s32[1,16,16]{2,1,0:T(8,128)} %occupancy_ref.3) | copy-start | bytes 3076
  92.0 51.5 %copy-start.16 = (bf16[256,512]{1,0:T(8,128)(2,1)S(1)}, bf16[256,512]{1,0:T(8,128)(2,1)}, u32[]{:S(2)}) copy-start(bf16[256,512]{1,0:T(8,128)(2,1)} %constant.40.clone.refs_0_) | copy-start | bytes 786436
  92.0 51.5 %copy-start.18 = (bf16[256,512]{1,0:T(8,128)(2,1)S(1)}, bf16[256,512]{1,0:T(8,128)(2,1)}, u32[]{:S(2)}) copy-start(bf16[256,512]{1,0:T(8,128)(2,1)} %constant.41.clone.refs_1_) | copy-start | bytes 786436
  92.0 51.5 %copy-start.20 = (bf16[512,256]{1,0:T(8,128)(2,1)S(1)}, bf16[512,256]{1,0:T(8,128)(2,1)}, u32[]{:S(2)}) copy-start(bf16[512,256]{1,0:T(8,128)(2,1)} %constant.42.clone.refs_2_) | copy-start | bytes 786436
  92.1 51.5 %copy-start.22 = (bf16[512,256]{1,0:T(8,128)(2,1)S(1)}, bf16[512,256]{1,0:T(8,128)(2,1)}, u32[]{:S(2)}) copy-start(bf16[512,256]{1,0:T(8,128)(2,1)} %constant.43.clone.refs_3_) | copy-start | bytes 786436
  143.5 26.7 %copy-start.10 = (f32[3,1,128,128]{3,2,1,0:T(8,128)S(1)}, f32[3,1,128,128]{3,2,1,0:T(8,128)}, u32[]{:S(2)}) copy-start(f32[3,1,128,128]{3,2,1,0:T(8,128)} %get-tuple-element.4.field_ref) | copy-start | bytes 589828

commit v2 on v0

--- a/solution.py
+++ b/solution.py
@@ -9,6 +9,8 @@
 from jax.sharding import PartitionSpec as P
 
 BLOCK = 8
+LANES = 128
+BEHIND = 14000
 F32 = jnp.float32
 BF16 = jnp.bfloat16
 PARTS = 3
@@ -27,20 +29,34 @@
     return 2.0 * np.pi * phase / count_out
 
 
-def plane_tables(cells):
+def tables_of(cells, devices):
     angle = angles(cells, 2 * cells)
     cosine, sine = np.cos(angle), np.sin(angle)
-    table = np.block([[cosine, -sine], [sine, cosine]])
-    return halves_of(table) + halves_of(np.ascontiguousarray(table.T))
-
-
-def z_tables(cells, devices):
-    angle = angles(cells, 2 * cells)
-    per_owner = 2 * cells // devices
-    both = np.stack([np.cos(angle).T, -np.sin(angle).T])
-    both = both.reshape(2, devices, per_owner, cells).transpose(2, 0, 1, 3)
-    table = both.reshape(4 * cells, cells)
-    return halves_of(table) + halves_of(np.ascontiguousarray(table.T) / float((2 * cells) ** 3))
+    plane = np.block([[cosine, -sine], [sine, cosine]])
+    both = np.stack([cosine.T, -sine.T]).reshape(2, devices, 2 * cells // devices, cells)
+    along_z = both.transpose(2, 0, 1, 3).reshape(4 * cells, cells)
+    return (along_z, along_z.T / float((2 * cells) ** 3), plane, plane.T)
+
+
+def packed_tables(cells, devices):
+    blocks, where, row = [], [], 0
+    for table in tables_of(cells, devices):
+        rows, columns = table.shape
+        for half in halves_of(table):
+            where.append((row, rows, columns))
+            for start in range(0, columns, LANES):
+                blocks.append(half[:, start : start + LANES])
+                row += rows
+    return np.concatenate(blocks, axis=0), where
+
+
+def table_from(tables_ref, entry):
+    def half(row, rows, columns):
+        return jnp.concatenate(
+            [tables_ref[row + i * rows : row + (i + 1) * rows] for i in range(columns // LANES)], axis=1
+        )
+
+    return tuple(half(*one) for one in entry)
 
 
 def split(value):
@@ -73,15 +89,19 @@
             out_ref[pl.ds(piece, devices, stride=PIECES), :] = spread[start : start + devices]
 
 
-def forward_z_kernel(field_ref, occupancy_ref, high_ref, low_ref, out_ref):
+def forward_z_kernel(field_ref, occupancy_ref, tables_ref, green_ref, out_ref, *, where):
     cells = field_ref.shape[-1]
     devices = out_ref.shape[0] // PIECES
     mask = mask_of(occupancy_ref[0], cells)
-    table = (high_ref[...], low_ref[...])
+    table = table_from(tables_ref, where[0:2])
     for part in range(PARTS):
         masked = split(field_ref[part, 0] * mask)
         spread = dot3(table, masked, ((1,), (1,)))
         put_pieces(out_ref, part, spread, devices)
+
+    @pl.when(lax.axis_index("comp") == 1)
+    def _():
+        pl.delay(BEHIND)
 
 
 def image_of(part, data_ref, field_ref, inverse_ref, mask, table, devices):
@@ -95,14 +115,12 @@
     return inverse_ref[0] * masked - mask * convolved
 
 
-def middle_z_kernel(
-    data_ref, field_ref, inverse_ref, occupancy_ref, high_ref, low_ref, back_high_ref, back_low_ref, image_ref, out_ref
-):
+def middle_z_kernel(data_ref, field_ref, inverse_ref, occupancy_ref, tables_ref, image_ref, out_ref, *, where):
     cells = field_ref.shape[-1]
     devices = out_ref.shape[0] // PIECES
     mask = mask_of(occupancy_ref[0], cells)
-    table = (high_ref[...], low_ref[...])
-    back = (back_high_ref[...], back_low_ref[...])
+    table = table_from(tables_ref, where[0:2])
+    back = table_from(tables_ref, where[2:4])
     for part in range(PARTS):
         image = image_of(part, data_ref, field_ref, inverse_ref, mask, back, devices)
         image_ref[part, 0] = image
@@ -110,21 +128,21 @@
         put_pieces(out_ref, part, spread, devices)
 
 
-def last_z_kernel(data_ref, field_ref, inverse_ref, occupancy_ref, back_high_ref, back_low_ref, image_ref):
+def last_z_kernel(data_ref, field_ref, inverse_ref, occupancy_ref, tables_ref, image_ref, *, where):
     cells = field_ref.shape[-1]
     devices = data_ref.shape[0] // PIECES
     mask = mask_of(occupancy_ref[0], cells)
-    back = (back_high_ref[...], back_low_ref[...])
+    back = table_from(tables_ref, where[2:4])
     for part in range(PARTS):
         image_ref[part, 0] = image_of(part, data_ref, field_ref, inverse_ref, mask, back, devices)
 
 
-def plane_kernel(data_ref, green_ref, high_ref, low_ref, t_high_ref, t_low_ref, out_ref, spectrum_ref):
+def plane_kernel(data_ref, green_ref, tables_ref, out_ref, spectrum_ref, *, where):
     devices = data_ref.shape[0] // PIECES
     length = green_ref.shape[-1]
     combos = ((0, 3, 4), (3, 1, 5), (4, 5, 2))
-    table = (high_ref[...], low_ref[...])
-    table_t = (t_high_ref[...], t_low_ref[...])
+    table = table_from(tables_ref, where[4:6])
+    table_t = table_from(tables_ref, where[6:8])
     for plane in range(PLANES):
 
         def piece_of(part, kind):
@@ -156,7 +174,7 @@
 VMEM = pl.BlockSpec(memory_space=pltpu.VMEM)
 
 
-def call(kernel, outs, args, flops, scratch=()):
+def call(kernel, outs, args, flops, scratch=(), mebibytes=12):
     single = not isinstance(outs, tuple)
     moved = sum(a.size * a.dtype.itemsize for a in args)
     return pl.pallas_call(
@@ -166,7 +184,7 @@
         out_specs=VMEM if single else (VMEM,) * len(outs),
         scratch_shapes=list(scratch),
         cost_estimate=pl.CostEstimate(flops=flops, bytes_accessed=moved, transcendentals=0),
-        compiler_params=pltpu.CompilerParams(vmem_limit_bytes=48 * 1024 * 1024),
+        compiler_params=pltpu.CompilerParams(vmem_limit_bytes=mebibytes * 1024 * 1024),
     )(*args)
 
 
@@ -180,31 +198,31 @@
 def per_device(devices, polarization, inverse_polarizability, occupancy, green_fourier):
     cells = polarization.shape[-1]
     length = green_fourier.shape[-1]
-    z_high, z_low, back_high, back_low = (jnp.asarray(t) for t in z_tables(cells, devices))
-    planes = tuple(jnp.asarray(t) for t in plane_tables(cells))
+    packed, where = packed_tables(cells, devices)
+    tables = jnp.asarray(packed)
     sent = jax.ShapeDtypeStruct((devices * PIECES, cells), F32)
     image = jax.ShapeDtypeStruct(polarization.shape, F32)
     z_flops = 3 * 2 * PARTS * cells * cells * 2 * length
     plane_flops = 3 * 2 * PARTS * PLANES * (4 * cells * cells * length + 4 * cells * length * length) * 2
 
+    def using(kernel):
+        return functools.partial(kernel, where=where)
+
     def planes_of(data):
         scratch = (pltpu.VMEM((PARTS, 2 * length, length), F32),)
-        return call(plane_kernel, sent, (data, green_fourier) + planes, plane_flops, scratch)
-
-    data = call(forward_z_kernel, sent, (polarization, occupancy, z_high, z_low), z_flops)
+        return call(using(plane_kernel), sent, (data, green_fourier, tables), plane_flops, scratch)
+
+    data = call(using(forward_z_kernel), sent, (polarization, occupancy, tables, green_fourier), z_flops)
     data = exchange(planes_of(exchange(data, devices)), devices)
     first_image, data = call(
-        middle_z_kernel,
+        using(middle_z_kernel),
         (image, sent),
-        (data, polarization, inverse_polarizability, occupancy, z_high, z_low, back_high, back_low),
+        (data, polarization, inverse_polarizability, occupancy, tables),
         2 * z_flops,
     )
     data = exchange(planes_of(exchange(data, devices)), devices)
     second_image = call(
-        last_z_kernel,
-        image,
-        (data, first_image, inverse_polarizability, occupancy, back_high, back_low),
-        z_flops,
+        using(last_z_kernel), image, (data, first_image, inverse_polarizability, occupancy, tables), z_flops
     )
     return (first_image, second_image)
 

time: 161 us -> 141 us (0.88); the launches traced: 158 us -> 141 us
  blocking collectives: 131 us -> 118 us
  local copies, waits for them, and re-layouts: 9.17 us -> 4.93 us
    all_to_all x4, blocking collectives: 131 us -> 118 us  [exchange(): lax.all_to_all(flat, 'slab', split_axis=0, concat_axis=0, tiled=True)]
    unnamed x40 -> x18, local copies, waits for them, and re-layouts: 9.17 us -> 4.93 us
where the time goes in v2:
time: 141 us
  blocking collectives  118 us (84%)
  Pallas kernels  17.3 us (12%)
  local copies, waits for them, and re-layouts  4.93 us (3%)
    all_to_all x4, blocking collectives, exchange(): lax.all_to_all(flat, 'slab', split_axis=0, concat_axis=0, tiled=True)  118 us
    pallas_call x5, Pallas kernels, call(): pl.pallas_call(kernel, out_shape=outs, in_specs=[VMEM] * len(args), out_s...  17.3 us
    unnamed x18, local copies, waits for them, and re-layouts  4.93 us

profile of v2, /device:TPU:1, one launch (start us, length us, event | category | flops | bytes accessed | tf_op | source)
XLA Modules:
  0.0 141.0 jit_solution(12987086331113790081)
XLA Ops:
  0.6 0.0 copy-start
  0.6 1.4 copy-done
  2.0 0.0 copy-start.2
  2.0 1.9 %copy-done.2 = f32[6,2,256,256]{3,2,1,0:T(8,128)S(1)} copy-done((f32[6,2,256,256]{3,2,1,0:T(8,128)S(1)}, f32[6,2,256,256]{3,2,1,0:T(8,128)}, u32[]{:S(2)}) %copy-start.2) | copy-done | bytes 3145752
  3.9 0.0 copy-start.4
  3.9 0.9 copy-done.4
  4.9 0.0 copy-start.7
  4.9 0.7 copy-done.7
  5.6 0.0 copy-start.1
  5.6 0.0 copy-start.3
  5.6 0.7 shard_map.68
  6.3 48.1 %all_to_all.20 = f32[128,1,1536]{2,1,0:T(1,128)S(1)} all-to-all(f32[128,1,1536]{2,1,0:T(1,128)S(1)} %bitcast.10), channel_id=1, replica_groups=mesh['slab'=128,'comp'=2] {'slab'}, dimensions={0} | all-to-all | bytes 1572864 | tf_op jit(solution)/shard_map/all_to_all | solution.py:194
  54.3 0.0 copy-done.1
  54.3 0.0 copy-done.3
  54.4 0.0 copy-start.5
  54.4 0.0 copy-start.8
  54.4 6.7 %shard_map.69 = f32[1536,128]{1,0:T(8,128)S(1)} custom-call(f32[1536,128]{1,0:T(8,128)S(1)} %bitcast.12, f32[6,2,256,256]{3,2,1,0:T(8,128)S(1)} %copy-done.3, bf16[6144,128]{1,0:T(8,128)(2,1)S(1)} %copy-done.1), custom_call_target="tpu_custom_call" | custom-call | flops 3623878656 | bytes 5505024 | tf_op jit(solution)/shard_map/pallas_call | solution.py:180
  61.1 23.5 %all_to_all.21 = f32[128,1,1536]{2,1,0:T(1,128)S(1)} all-to-all(f32[128,1,1536]{2,1,0:T(1,128)S(1)} %bitcast.13), channel_id=1, replica_groups=mesh['slab'=128,'comp'=2] {'slab'}, dimensions={0} | all-to-all | bytes 1572864 | tf_op jit(solution)/shard_map/all_to_all | solution.py:194
  84.6 0.0 copy-done.5
  84.6 0.0 copy-done.8
  84.6 1.8 %shard_map.70 = (f32[3,1,128,128]{3,2,1,0:T(8,128)}, f32[1536,128]{1,0:T(8,128)S(1)}) custom-call(f32[1536,128]{1,0:T(8,128)S(1)} %bitcast.8, f32[3,1,128,128]{3,2,1,0:T(8,128)S(1)} %copy-done.4, f32[1,128,128]{2,1,0:T(8,128)S(1)} %copy-done.5, s32[1,16,16]{2,1,0:T(8,128)S(1)} %copy-done.8, bf16[6144,128]{1,0:T(8,128)(2,1)S(1)} %copy-done.1), custom_call_target="tpu_custom_call" | custom-call | flops 301989888 | bytes 2622464 | tf_op jit(solution)/shard_map/pallas_call | solution.py:180
  86.4 23.4 %all_to_all.22 = f32[128,1,1536]{2,1,0:T(1,128)S(1)} all-to-all(f32[128,1,1536]{2,1,0:T(1,128)S(1)} %bitcast.11), channel_id=1, replica_groups=mesh['slab'=128,'comp'=2] {'slab'}, dimensions={0} | all-to-all | bytes 1572864 | tf_op jit(solution)/shard_map/all_to_all | solution.py:194
  109.8 0.0 copy-start.6
  109.8 6.7 %shard_map.71 = f32[1536,128]{1,0:T(8,128)S(1)} custom-call(f32[1536,128]{1,0:T(8,128)S(1)} %bitcast.14, f32[6,2,256,256]{3,2,1,0:T(8,128)S(1)} %copy-done.3, bf16[6144,128]{1,0:T(8,128)(2,1)S(1)} %copy-done.1), custom_call_target="tpu_custom_call" | custom-call | flops 3623878656 | bytes 5505024 | tf_op jit(solution)/shard_map/pallas_call | solution.py:180
  116.5 23.2 %all_to_all.23 = f32[128,1,1536]{2,1,0:T(1,128)S(1)} all-to-all(f32[128,1,1536]{2,1,0:T(1,128)S(1)} %bitcast.15), channel_id=1, replica_groups=mesh['slab'=128,'comp'=2] {'slab'}, dimensions={0} | all-to-all | bytes 1572864 | tf_op jit(solution)/shard_map/all_to_all | solution.py:194
  139.7 0.0 copy-done.6
  139.7 1.3 shard_map.72
Async XLA Ops:
  0.6 1.4 %copy-start = (bf16[6144,128]{1,0:T(8,128)(2,1)S(1)}, bf16[6144,128]{1,0:T(8,128)(2,1)}, u32[]{:S(2)}) copy-start(bf16[6144,128]{1,0:T(8,128)(2,1)} %constant.2.clone.tables_ref) | copy-start | bytes 4718596
  2.0 1.9 %copy-start.2 = (f32[6,2,256,256]{3,2,1,0:T(8,128)S(1)}, f32[6,2,256,256]{3,2,1,0:T(8,128)}, u32[]{:S(2)}) copy-start(f32[6,2,256,256]{3,2,1,0:T(8,128)} %green_ref.5) | copy-start | bytes 9437188
  3.9 0.9 copy-start.4
  4.9 0.7 copy-start.7
  5.6 48.8 %copy-start.1 = (bf16[6144,128]{1,0:T(8,128)(2,1)S(1)}, bf16[6144,128]{1,0:T(8,128)(2,1)}, u32[]{:S(2)}) copy-start(bf16[6144,128]{1,0:T(8,128)(2,1)} %constant.2.clone.tables_ref) | copy-start | bytes 4718596
  5.6 48.8 %copy-start.3 = (f32[6,2,256,256]{3,2,1,0:T(8,128)S(1)}, f32[6,2,256,256]{3,2,1,0:T(8,128)}, u32[]{:S(2)}) copy-start(f32[6,2,256,256]{3,2,1,0:T(8,128)} %green_ref.5) | copy-start | bytes 9437188
  54.4 30.2 %copy-start.5 = (f32[1,128,128]{2,1,0:T(8,128)S(1)}, f32[1,128,128]{2,1,0:T(8,128)}, u32[]{:S(2)}) copy-start(f32[1,128,128]{2,1,0:T(8,128)} %inverse_ref.3) | copy-start | bytes 196612
  54.4 30.2 %copy-start.8 = (s32[1,16,16]{2,1,0:T(8,128)S(1)}, s32[1,16,16]{2,1,0:T(8,128)}, u32[]{:S(2)}) copy-start(s32[1,16,16]{2,1,0:T(8,128)} %occupancy_ref.5) | copy-start | bytes 3076
  109.8 29.9 %copy-start.6 = (f32[3,1,128,128]{3,2,1,0:T(8,128)S(1)}, f32[3,1,128,128]{3,2,1,0:T(8,128)}, u32[]{:S(2)}) copy-start(f32[3,1,128,128]{3,2,1,0:T(8,128)} %get-tuple-element.2.field_ref) | copy-start | bytes 589828

commit v3 on v2

--- a/solution.py
+++ b/solution.py
@@ -68,7 +68,9 @@
     def one(a, b):
         return lax.dot_general(a, b, (dims, ((), ())), preferred_element_type=F32)
 
-    return one(left[0], right[0]) + one(left[1], right[0]) + one(left[0], right[1])
+    rows = left[0].shape[0]
+    both = one(jnp.concatenate(left, axis=0), right[0])
+    return both[:rows] + both[rows:] + one(left[0], right[1])
 
 
 def mask_of(occupancy, cells):
@@ -148,11 +150,16 @@
         def piece_of(part, kind):
             return pl.ds((part * PLANES + plane) * 2 + kind, devices, stride=PIECES)
 
+        rows = [
+            jnp.concatenate([data_ref[piece_of(part, 0), :], data_ref[piece_of(part, 1), :]], axis=1)
+            for part in range(PARTS)
+        ]
+        along_y = dot3(split(jnp.concatenate(rows, axis=0)), table)
         for part in range(PARTS):
-            rows = jnp.concatenate([data_ref[piece_of(part, 0), :], data_ref[piece_of(part, 1), :]], axis=1)
-            along_y = dot3(split(rows), table)
-            stacked = jnp.concatenate([along_y[:, :length], along_y[:, length:]], axis=0)
+            here = along_y[part * devices : (part + 1) * devices]
+            stacked = jnp.concatenate([here[:, :length], here[:, length:]], axis=0)
             spectrum_ref[part] = dot3(table_t, split(stacked))
+        rows = []
         for part in range(PARTS):
             row = combos[part]
             first, second, third = green_ref[row[0], plane], green_ref[row[1], plane], green_ref[row[2], plane]
@@ -165,10 +172,12 @@
 
             field = jnp.concatenate([product(0), product(1)], axis=0)
             along_x = dot3(table, split(field))
-            rows = jnp.concatenate([along_x[:devices], along_x[devices:]], axis=1)
-            back = dot3(split(rows), table_t)
-            out_ref[piece_of(part, 0), :] = back[:, :devices]
-            out_ref[piece_of(part, 1), :] = back[:, devices:]
+            rows.append(jnp.concatenate([along_x[:devices], along_x[devices:]], axis=1))
+        back = dot3(split(jnp.concatenate(rows, axis=0)), table_t)
+        for part in range(PARTS):
+            here = back[part * devices : (part + 1) * devices]
+            out_ref[piece_of(part, 0), :] = here[:, :devices]
+            out_ref[piece_of(part, 1), :] = here[:, devices:]
 
 
 VMEM = pl.BlockSpec(memory_space=pltpu.VMEM)

time: 141 us -> 139 us (0.986)
  Pallas kernels: 17.3 us -> 14.7 us
    pallas_call x5, Pallas kernels: 17.3 us -> 14.7 us  [call(): pl.pallas_call(kernel, out_shape=outs, in_specs=[VMEM] * len(args), out_s...]
where the time goes in v3:
time: 139 us; the launch traced here: 138 us
  blocking collectives  118 us (85%)
  Pallas kernels  14.7 us (11%)
  local copies, waits for them, and re-layouts  4.93 us (4%)
    all_to_all x4, blocking collectives, exchange(): lax.all_to_all(flat, 'slab', split_axis=0, concat_axis=0, tiled=True)  118 us
    pallas_call x5, Pallas kernels, call(): pl.pallas_call(kernel, out_shape=outs, in_specs=[VMEM] * len(args), out_s...  14.7 us
    unnamed x18, local copies, waits for them, and re-layouts  4.93 us

profile of v3, /device:TPU:1, one launch (start us, length us, event | category | flops | bytes accessed | tf_op | source)
XLA Modules:
  0.0 138.3 jit_solution(1694201109189163987)
XLA Ops:
  0.6 0.0 copy-start
  0.6 1.4 %copy-done = bf16[6144,128]{1,0:T(8,128)(2,1)S(1)} copy-done((bf16[6144,128]{1,0:T(8,128)(2,1)S(1)}, bf16[6144,128]{1,0:T(8,128)(2,1)}, u32[]{:S(2)}) %copy-start) | copy-done | bytes 1572888
  2.0 0.0 copy-start.2
  2.0 1.9 %copy-done.2 = f32[6,2,256,256]{3,2,1,0:T(8,128)S(1)} copy-done((f32[6,2,256,256]{3,2,1,0:T(8,128)S(1)}, f32[6,2,256,256]{3,2,1,0:T(8,128)}, u32[]{:S(2)}) %copy-start.2) | copy-done | bytes 3145752
  3.9 0.0 copy-start.4
  3.9 0.9 copy-done.4
  4.9 0.0 copy-start.7
  4.9 0.7 copy-done.7
  5.6 0.0 copy-start.1
  5.6 0.0 copy-start.3
  5.6 0.7 shard_map.68
  6.3 48.1 %all_to_all.20 = f32[128,1,1536]{2,1,0:T(1,128)S(1)} all-to-all(f32[128,1,1536]{2,1,0:T(1,128)S(1)} %bitcast.10), channel_id=1, replica_groups=mesh['slab'=128,'comp'=2] {'slab'}, dimensions={0} | all-to-all | bytes 1572864 | tf_op jit(solution)/shard_map/all_to_all | solution.py:203
  54.3 0.0 copy-done.1
  54.3 0.0 copy-done.3
  54.4 0.0 copy-start.5
  54.4 0.0 copy-start.8
  54.4 5.5 %shard_map.69 = f32[1536,128]{1,0:T(8,128)S(1)} custom-call(f32[1536,128]{1,0:T(8,128)S(1)} %bitcast.12, f32[6,2,256,256]{3,2,1,0:T(8,128)S(1)} %copy-done.3, bf16[6144,128]{1,0:T(8,128)(2,1)S(1)} %copy-done.1), custom_call_target="tpu_custom_call" | custom-call | flops 3623878656 | bytes 5505024 | tf_op jit(solution)/shard_map/pallas_call | solution.py:189
  59.8 23.5 %all_to_all.21 = f32[128,1,1536]{2,1,0:T(1,128)S(1)} all-to-all(f32[128,1,1536]{2,1,0:T(1,128)S(1)} %bitcast.13), channel_id=1, replica_groups=mesh['slab'=128,'comp'=2] {'slab'}, dimensions={0} | all-to-all | bytes 1572864 | tf_op jit(solution)/shard_map/all_to_all | solution.py:203
  83.3 0.0 copy-done.5
  83.3 0.0 copy-done.8
  83.3 1.8 %shard_map.70 = (f32[3,1,128,128]{3,2,1,0:T(8,128)}, f32[1536,128]{1,0:T(8,128)S(1)}) custom-call(f32[1536,128]{1,0:T(8,128)S(1)} %bitcast.8, f32[3,1,128,128]{3,2,1,0:T(8,128)S(1)} %copy-done.4, f32[1,128,128]{2,1,0:T(8,128)S(1)} %copy-done.5, s32[1,16,16]{2,1,0:T(8,128)S(1)} %copy-done.8, bf16[6144,128]{1,0:T(8,128)(2,1)S(1)} %copy-done.1), custom_call_target="tpu_custom_call" | custom-call | flops 301989888 | bytes 2622464 | tf_op jit(solution)/shard_map/pallas_call | solution.py:189
  85.1 23.2 %all_to_all.22 = f32[128,1,1536]{2,1,0:T(1,128)S(1)} all-to-all(f32[128,1,1536]{2,1,0:T(1,128)S(1)} %bitcast.11), channel_id=1, replica_groups=mesh['slab'=128,'comp'=2] {'slab'}, dimensions={0} | all-to-all | bytes 1572864 | tf_op jit(solution)/shard_map/all_to_all | solution.py:203
  108.3 0.0 copy-start.6
  108.3 5.5 %shard_map.71 = f32[1536,128]{1,0:T(8,128)S(1)} custom-call(f32[1536,128]{1,0:T(8,128)S(1)} %bitcast.14, f32[6,2,256,256]{3,2,1,0:T(8,128)S(1)} %copy-done.3, bf16[6144,128]{1,0:T(8,128)(2,1)S(1)} %copy-done.1), custom_call_target="tpu_custom_call" | custom-call | flops 3623878656 | bytes 5505024 | tf_op jit(solution)/shard_map/pallas_call | solution.py:189
  113.8 23.2 %all_to_all.23 = f32[128,1,1536]{2,1,0:T(1,128)S(1)} all-to-all(f32[128,1,1536]{2,1,0:T(1,128)S(1)} %bitcast.15), channel_id=1, replica_groups=mesh['slab'=128,'comp'=2] {'slab'}, dimensions={0} | all-to-all | bytes 1572864 | tf_op jit(solution)/shard_map/all_to_all | solution.py:203
  137.0 0.0 copy-done.6
  137.0 1.3 shard_map.72
Async XLA Ops:
  0.6 1.4 %copy-start = (bf16[6144,128]{1,0:T(8,128)(2,1)S(1)}, bf16[6144,128]{1,0:T(8,128)(2,1)}, u32[]{:S(2)}) copy-start(bf16[6144,128]{1,0:T(8,128)(2,1)} %constant.2.clone.tables_ref) | copy-start | bytes 4718596
  2.0 1.9 %copy-start.2 = (f32[6,2,256,256]{3,2,1,0:T(8,128)S(1)}, f32[6,2,256,256]{3,2,1,0:T(8,128)}, u32[]{:S(2)}) copy-start(f32[6,2,256,256]{3,2,1,0:T(8,128)} %green_ref.5) | copy-start | bytes 9437188
  3.9 0.9 copy-start.4
  4.9 0.7 copy-start.7
  5.6 48.8 %copy-start.1 = (bf16[6144,128]{1,0:T(8,128)(2,1)S(1)}, bf16[6144,128]{1,0:T(8,128)(2,1)}, u32[]{:S(2)}) copy-start(bf16[6144,128]{1,0:T(8,128)(2,1)} %constant.2.clone.tables_ref) | copy-start | bytes 4718596
  5.6 48.8 %copy-start.3 = (f32[6,2,256,256]{3,2,1,0:T(8,128)S(1)}, f32[6,2,256,256]{3,2,1,0:T(8,128)}, u32[]{:S(2)}) copy-start(f32[6,2,256,256]{3,2,1,0:T(8,128)} %green_ref.5) | copy-start | bytes 9437188
  54.4 29.0 %copy-start.5 = (f32[1,128,128]{2,1,0:T(8,128)S(1)}, f32[1,128,128]{2,1,0:T(8,128)}, u32[]{:S(2)}) copy-start(f32[1,128,128]{2,1,0:T(8,128)} %inverse_ref.3) | copy-start | bytes 196612
  54.4 29.0 %copy-start.8 = (s32[1,16,16]{2,1,0:T(8,128)S(1)}, s32[1,16,16]{2,1,0:T(8,128)}, u32[]{:S(2)}) copy-start(s32[1,16,16]{2,1,0:T(8,128)} %occupancy_ref.5) | copy-start | bytes 3076
  108.3 28.7 %copy-start.6 = (f32[3,1,128,128]{3,2,1,0:T(8,128)S(1)}, f32[3,1,128,128]{3,2,1,0:T(8,128)}, u32[]{:S(2)}) copy-start(f32[3,1,128,128]{3,2,1,0:T(8,128)} %get-tuple-element.2.field_ref) | copy-start | bytes 589828

commit v4 on v3

--- a/solution.py
+++ b/solution.py
@@ -10,7 +10,7 @@
 
 BLOCK = 8
 LANES = 128
-BEHIND = 14000
+BEHIND = 13000
 F32 = jnp.float32
 BF16 = jnp.bfloat16
 PARTS = 3

time: 139 us -> 138 us (level)
  no operation moved by 1% of the time
where the time goes in v4:
time: 138 us
  blocking collectives  118 us (86%)
  Pallas kernels  14.7 us (11%)
  local copies, waits for them, and re-layouts  4.93 us (4%)
    all_to_all x4, blocking collectives, exchange(): lax.all_to_all(flat, 'slab', split_axis=0, concat_axis=0, tiled=True)  118 us
    pallas_call x5, Pallas kernels, call(): pl.pallas_call(kernel, out_shape=outs, in_specs=[VMEM] * len(args), out_s...  14.7 us
    unnamed x18, local copies, waits for them, and re-layouts  4.93 us

profile of v4, /device:TPU:1, one launch (start us, length us, event | category | flops | bytes accessed | tf_op | source)
XLA Modules:
  0.0 137.9 jit_solution(189552482285268344)
XLA Ops:
  0.6 0.0 copy-start
  0.6 1.4 %copy-done = bf16[6144,128]{1,0:T(8,128)(2,1)S(1)} copy-done((bf16[6144,128]{1,0:T(8,128)(2,1)S(1)}, bf16[6144,128]{1,0:T(8,128)(2,1)}, u32[]{:S(2)}) %copy-start) | copy-done | bytes 1572888
  2.0 0.0 copy-start.2
  2.0 1.9 %copy-done.2 = f32[6,2,256,256]{3,2,1,0:T(8,128)S(1)} copy-done((f32[6,2,256,256]{3,2,1,0:T(8,128)S(1)}, f32[6,2,256,256]{3,2,1,0:T(8,128)}, u32[]{:S(2)}) %copy-start.2) | copy-done | bytes 3145752
  3.9 0.0 copy-start.4
  3.9 0.9 copy-done.4
  4.9 0.0 copy-start.7
  4.9 0.7 copy-done.7
  5.6 0.0 copy-start.1
  5.6 0.0 copy-start.3
  5.6 0.7 shard_map.68
  6.3 47.1 %all_to_all.20 = f32[128,1,1536]{2,1,0:T(1,128)S(1)} all-to-all(f32[128,1,1536]{2,1,0:T(1,128)S(1)} %bitcast.10), channel_id=1, replica_groups=mesh['slab'=128,'comp'=2] {'slab'}, dimensions={0} | all-to-all | bytes 1572864 | tf_op jit(solution)/shard_map/all_to_all | solution.py:203
  53.4 0.0 copy-done.1
  53.4 0.0 copy-done.3
  53.4 0.0 copy-start.5
  53.4 0.0 copy-start.8
  53.4 5.5 %shard_map.69 = f32[1536,128]{1,0:T(8,128)S(1)} custom-call(f32[1536,128]{1,0:T(8,128)S(1)} %bitcast.12, f32[6,2,256,256]{3,2,1,0:T(8,128)S(1)} %copy-done.3, bf16[6144,128]{1,0:T(8,128)(2,1)S(1)} %copy-done.1), custom_call_target="tpu_custom_call" | custom-call | flops 3623878656 | bytes 5505024 | tf_op jit(solution)/shard_map/pallas_call | solution.py:189
  58.8 23.2 %all_to_all.21 = f32[128,1,1536]{2,1,0:T(1,128)S(1)} all-to-all(f32[128,1,1536]{2,1,0:T(1,128)S(1)} %bitcast.13), channel_id=1, replica_groups=mesh['slab'=128,'comp'=2] {'slab'}, dimensions={0} | all-to-all | bytes 1572864 | tf_op jit(solution)/shard_map/all_to_all | solution.py:203
  82.0 0.0 copy-done.5
  82.1 0.0 copy-done.8
  82.1 1.8 %shard_map.70 = (f32[3,1,128,128]{3,2,1,0:T(8,128)}, f32[1536,128]{1,0:T(8,128)S(1)}) custom-call(f32[1536,128]{1,0:T(8,128)S(1)} %bitcast.8, f32[3,1,128,128]{3,2,1,0:T(8,128)S(1)} %copy-done.4, f32[1,128,128]{2,1,0:T(8,128)S(1)} %copy-done.5, s32[1,16,16]{2,1,0:T(8,128)S(1)} %copy-done.8, bf16[6144,128]{1,0:T(8,128)(2,1)S(1)} %copy-done.1), custom_call_target="tpu_custom_call" | custom-call | flops 301989888 | bytes 2622464 | tf_op jit(solution)/shard_map/pallas_call | solution.py:189
  83.9 23.3 %all_to_all.22 = f32[128,1,1536]{2,1,0:T(1,128)S(1)} all-to-all(f32[128,1,1536]{2,1,0:T(1,128)S(1)} %bitcast.11), channel_id=1, replica_groups=mesh['slab'=128,'comp'=2] {'slab'}, dimensions={0} | all-to-all | bytes 1572864 | tf_op jit(solution)/shard_map/all_to_all | solution.py:203
  107.1 0.0 copy-start.6
  107.1 5.5 %shard_map.71 = f32[1536,128]{1,0:T(8,128)S(1)} custom-call(f32[1536,128]{1,0:T(8,128)S(1)} %bitcast.14, f32[6,2,256,256]{3,2,1,0:T(8,128)S(1)} %copy-done.3, bf16[6144,128]{1,0:T(8,128)(2,1)S(1)} %copy-done.1), custom_call_target="tpu_custom_call" | custom-call | flops 3623878656 | bytes 5505024 | tf_op jit(solution)/shard_map/pallas_call | solution.py:189
  112.6 24.0 %all_to_all.23 = f32[128,1,1536]{2,1,0:T(1,128)S(1)} all-to-all(f32[128,1,1536]{2,1,0:T(1,128)S(1)} %bitcast.15), channel_id=1, replica_groups=mesh['slab'=128,'comp'=2] {'slab'}, dimensions={0} | all-to-all | bytes 1572864 | tf_op jit(solution)/shard_map/all_to_all | solution.py:203
  136.6 0.0 copy-done.6
  136.6 1.3 shard_map.72
Async XLA Ops:
  0.6 1.4 %copy-start = (bf16[6144,128]{1,0:T(8,128)(2,1)S(1)}, bf16[6144,128]{1,0:T(8,128)(2,1)}, u32[]{:S(2)}) copy-start(bf16[6144,128]{1,0:T(8,128)(2,1)} %constant.2.clone.tables_ref) | copy-start | bytes 4718596
  2.0 1.9 %copy-start.2 = (f32[6,2,256,256]{3,2,1,0:T(8,128)S(1)}, f32[6,2,256,256]{3,2,1,0:T(8,128)}, u32[]{:S(2)}) copy-start(f32[6,2,256,256]{3,2,1,0:T(8,128)} %green_ref.5) | copy-start | bytes 9437188
  3.9 0.9 copy-start.4
  4.9 0.7 copy-start.7
  5.6 47.8 %copy-start.1 = (bf16[6144,128]{1,0:T(8,128)(2,1)S(1)}, bf16[6144,128]{1,0:T(8,128)(2,1)}, u32[]{:S(2)}) copy-start(bf16[6144,128]{1,0:T(8,128)(2,1)} %constant.2.clone.tables_ref) | copy-start | bytes 4718596
  5.6 47.8 %copy-start.3 = (f32[6,2,256,256]{3,2,1,0:T(8,128)S(1)}, f32[6,2,256,256]{3,2,1,0:T(8,128)}, u32[]{:S(2)}) copy-start(f32[6,2,256,256]{3,2,1,0:T(8,128)} %green_ref.5) | copy-start | bytes 9437188
  53.4 28.7 %copy-start.5 = (f32[1,128,128]{2,1,0:T(8,128)S(1)}, f32[1,128,128]{2,1,0:T(8,128)}, u32[]{:S(2)}) copy-start(f32[1,128,128]{2,1,0:T(8,128)} %inverse_ref.3) | copy-start | bytes 196612
  53.4 28.7 %copy-start.8 = (s32[1,16,16]{2,1,0:T(8,128)S(1)}, s32[1,16,16]{2,1,0:T(8,128)}, u32[]{:S(2)}) copy-start(s32[1,16,16]{2,1,0:T(8,128)} %occupancy_ref.5) | copy-start | bytes 3076
  107.1 29.5 %copy-start.6 = (f32[3,1,128,128]{3,2,1,0:T(8,128)S(1)}, f32[3,1,128,128]{3,2,1,0:T(8,128)}, u32[]{:S(2)}) copy-start(f32[3,1,128,128]{3,2,1,0:T(8,128)} %get-tuple-element.2.field_ref) | copy-start | bytes 589828
